TPU v7x, 32 devices: a whole 2x2x4 slice. The times are simulated.
32 devices in a mesh: pipe: 4 (over y, core), tensor: 8 (over z, x).
Axes of the slice: x: 2, y: 2, z: 4, core: 2. Of those that a mesh axis runs over, the one named last changes fastest.
Arguments:
- patches: bfloat16 [16384, 1280], P(('pipe', 'tensor')), may hold values from -6 to 6
- attn_gain: float32 [1280], replicated, may hold values from 0.25 to 1.75
- w_qkv: bfloat16 [1280, 3840], P('tensor', 'pipe'), may hold values from -0.1118034 to 0.1118034
- w_out: bfloat16 [1280, 1280], P('tensor', 'pipe'), may hold values from -0.15625 to 0.15625
- merge_gain: float32 [1280], replicated, may hold values from 0.25 to 1.75
- window_ids: int32 [16384], P(('pipe', 'tensor')), may hold values from 0 to 127, as said below
- image_patches: int32 [128], P(('pipe', 'tensor')), may hold values from 0 to 512, as said below
- image_sample: int32 [128], P(('pipe', 'tensor')), may hold values from 0 to 7
Outputs:
- vision_seq: bfloat16 [4, 128, 8, 5120], P('pipe', None, 'tensor')
Inputs may be any that keep to these rules, and one draw needn't show every extreme that they name: `window_ids`: Non-decreasing within each bundle and equal over each 4 consecutive slots; every window lies within one aligned block of 64 slots of a bundle. `image_patches`: multiples of 128; the images of one bundle take at most 512 slots and at least half of them, and in every micro-batch some bundle is full.
All inputs are finite; a program needn't handle non-finite values.
Results may differ from a plain program's by a relative error of at most 0.0053.
Values may be sent and summed in bfloat16 or wider, within the bound.
A program may use at most 64 MiB of HBM per device.

v0:
```python
import math
import jax
import jax.numpy as jnp
from jax import lax
from jax.sharding import PartitionSpec as P

HEADS = 16
WINDOW = 64
SAMPLES = 8
epsilon = 1e-06


def normalize(values, gain_row):
    return (
        values * lax.rsqrt(jnp.mean(values * values, axis=-1, keepdims=True) + epsilon) * gain_row
    )


def token_positions(starts, merged_count, token_count):
    offsets = jnp.cumsum(merged_count) - merged_count
    token_index = jnp.arange(token_count, dtype=jnp.int32)
    inside = (token_index[None, :] >= offsets[:, None]) & (
        token_index[None, :] < (offsets + merged_count)[:, None]
    )
    position = jnp.sum(
        jnp.where(inside, starts[:, None] + token_index[None, :] - offsets[:, None], 0), axis=0
    )
    return jnp.where(jnp.any(inside, axis=0), position, -1)


def body(patches, attn_gain, w_qkv, w_out, merge_gain, window_ids, image_patches, image_sample):
    patch_count, feature_width = patches.shape
    token_count = patch_count // 4
    group_size = lax.axis_size("tensor")
    own_index = lax.axis_index("tensor")
    residual = patches.astype(jnp.float32)
    normed = normalize(residual, attn_gain).astype(jnp.bfloat16)
    qkv_rows = lax.all_gather(w_qkv, "tensor", axis=0, tiled=True)
    qkv = jnp.dot(
        normed,
        lax.all_gather(qkv_rows, "pipe", axis=1, tiled=True),
        preferred_element_type=jnp.float32,
    ).astype(jnp.bfloat16)
    head_width = feature_width // HEADS
    tile_count = patch_count // WINDOW

    def split_heads(block):
        return block.reshape(tile_count, WINDOW, HEADS, head_width)

    queries = split_heads(qkv[:, :feature_width])
    keys_tile = split_heads(qkv[:, feature_width : 2 * feature_width])
    values_tile = split_heads(qkv[:, 2 * feature_width :])
    scores = jnp.einsum(
        "tqhd,tkhd->thqk", queries, keys_tile, preferred_element_type=jnp.float32
    ) * (1.0 / math.sqrt(head_width))
    live_row = jnp.arange(patch_count, dtype=jnp.int32) < jnp.sum(image_patches)
    window_tile = window_ids.reshape(tile_count, WINDOW)
    live_tile = live_row.reshape(tile_count, WINDOW)
    allowed = (window_tile[:, :, None] == window_tile[:, None, :]) & live_tile[:, None, :]
    scores = jnp.where(allowed[:, None, :, :], scores, -1e30)
    row_max = jnp.max(scores, axis=-1, keepdims=True)
    exponent = jnp.exp(scores - row_max)
    weights = (exponent / jnp.sum(exponent, axis=-1, keepdims=True)).astype(jnp.bfloat16)
    context = jnp.einsum(
        "thqk,tkhd->tqhd", weights, values_tile, preferred_element_type=jnp.float32
    ).reshape(patch_count, feature_width)
    context = jnp.where(live_row[:, None], context, 0.0).astype(jnp.bfloat16)
    proj_rows = lax.all_gather(w_out, "tensor", axis=0, tiled=True)
    attended = jnp.dot(
        context,
        lax.all_gather(proj_rows, "pipe", axis=1, tiled=True),
        preferred_element_type=jnp.float32,
    )
    hidden = residual + attended
    merged = (
        normalize(hidden, merge_gain).astype(jnp.bfloat16).reshape(token_count, 4 * feature_width)
    )
    outgoing = merged.reshape(token_count // group_size, group_size, 4 * feature_width)
    merged_count = image_patches // 4
    sample_hot = image_sample[:, None] == jnp.arange(SAMPLES, dtype=jnp.int32)[None, :]
    sample_tally = jnp.sum(jnp.where(sample_hot, merged_count[:, None], 0), axis=0)
    all_tallies = lax.all_gather(sample_tally[None, :], "tensor", axis=0, tiled=True)
    source_ranks = jnp.arange(group_size, dtype=jnp.int32)
    before = jnp.sum(jnp.where((source_ranks < own_index)[:, None], all_tallies, 0), axis=0)
    totals = jnp.sum(all_tallies, axis=0)
    sample_index = jnp.arange(SAMPLES, dtype=jnp.int32)
    sample_base = jnp.sum(
        jnp.where(sample_index[None, :] < sample_index[:, None], totals[None, :], 0), axis=1
    )
    image_order = jnp.arange(image_sample.shape[0], dtype=jnp.int32)
    same_before = (image_sample[None, :] == image_sample[:, None]) & (
        image_order[None, :] < image_order[:, None]
    )
    earlier = jnp.sum(jnp.where(same_before, merged_count[None, :], 0), axis=1)
    starts = jnp.sum(jnp.where(sample_hot, (sample_base + before)[None, :], 0), axis=1) + earlier
    position = token_positions(starts, merged_count, token_count)
    outgoing_position = position.reshape(token_count // group_size, group_size)
    received, received_position = (
        lax.all_to_all(outgoing, "tensor", split_axis=1, concat_axis=0, tiled=True),
        lax.all_to_all(outgoing_position, "tensor", split_axis=1, concat_axis=0, tiled=True),
    )
    dest_rows = received_position.reshape(token_count) // group_size
    placement = (jnp.arange(token_count, dtype=jnp.int32)[:, None] == dest_rows[None, :]).astype(
        jnp.bfloat16
    )
    placed = jnp.dot(
        placement,
        received.reshape(token_count, 4 * feature_width),
        preferred_element_type=jnp.float32,
    )
    return placed.astype(jnp.bfloat16).reshape(1, token_count, 1, 4 * feature_width)


def solution(mesh):
    return jax.shard_map(
        body,
        mesh=mesh,
        in_specs=(
            P(("pipe", "tensor"), None),
            P(),
            P("tensor", "pipe"),
            P("tensor", "pipe"),
            P(),
            P(("pipe", "tensor")),
            P(("pipe", "tensor")),
            P(("pipe", "tensor")),
        ),
        out_specs=P("pipe", None, "tensor", None),
        check_vma=False,
    )
```

profile of v0, /device:TPU:0, one launch (start us, length us, event | category | flops | bytes accessed | tf_op | source)
XLA Modules:
  0.0 223.8 jit_solution(180956799762831658)
XLA Ops:
  6.5 0.7 all-gather.5.cloned.1.call-update
  7.3 59.4 %all-gather.5.cloned.1.call-done = bf16[1280,960]{1,0:T(8,128)(2,1)} async-done(((bf16[160,960]{1,0:T(8,128)(2,1)}), bf16[1280,960]{1,0:T(8,128)(2,1)}) %all-gather.5.cloned.1.call-update) | async-done | bytes 2457616 | tf_op jit(solution)/shard_map/all_gather | solution.py:38
  66.7 4.4 %copy.40 = bf16[1280,960]{0,1:T(8,128)(2,1)} copy(bf16[1280,960]{1,0:T(8,128)(2,1)} %all-gather.5.cloned.1.call-done) | data formatting | bytes 4915200 | tf_op jit(solution)/shard_map/all_gather | solution.py:38
  71.2 33.0 %all_gather.18 = bf16[1280,320]{1,0:T(8,128)(2,1)S(1)} all-gather(bf16[160,320]{1,0:T(8,128)(2,1)S(1)} %copy-done.3), channel_id=1, replica_groups=mesh['pipe'=4,'tensor'=8] {'tensor'}, dimensions={0}, use_global_device_ids=true | all-gather | bytes 921600 | tf_op jit(solution)/shard_map/all_gather | solution.py:68
  104.2 1.3 copy.46
  108.0 8.6 %all-reduce = s32[64]{0:T(128)S(1)} all-reduce(s32[64]{0:T(128)S(1)} %dynamic-update-slice), channel_id=2, replica_groups=mesh['pipe'=4,'tensor'=8] {'tensor'}, use_global_device_ids=true, to_apply=%add | all-reduce | flops 64 | bytes 512
  118.2 4.5 %all-to-all-start = ((s32[16,8,1]{0,2,1:T(1,128)}), s32[16,8,1]{0,2,1:T(1,128)S(1)}, u32[]{:S(2)}, u32[]{:S(2)}) async-start(s32[16,8,1]{0,2,1:T(1,128)} %copy.39), calls=%async_computation | async-start | bytes 8192 | tf_op jit(solution)/shard_map/all_to_all | solution.py:100
  124.7 11.6 %all-gather.7.cloned.1.call-done = bf16[1280,3840]{0,1:T(8,128)(2,1)} async-done(((bf16[1280,960]{0,1:T(8,128)(2,1)}), bf16[1280,3840]{0,1:T(8,128)(2,1)}) %all-gather.7.cloned.1.call-update) | async-done | bytes 9830416 | tf_op jit(solution)/shard_map/all_gather | solution.py:41
  136.3 9.5 %convolution_convert_fusion.1 = bf16[512,3840]{1,0:T(8,128)(2,1)S(1)} fusion(bf16[1280,3840]{0,1:T(8,128)(2,1)} %all-gather.7.cloned.1.call-done, bf16[512,1280]{1,0:T(8,128)(2,1)S(1)} %copy-done.1, f32[1280]{0:T(1024)S(1)} %copy-done.7, f32[512]{0:T(512)S(1)} %add_rsqrt_fusion.1), kind=kOutput, calls=%fused_computation.2 | convolution fusion | flops 5037752320 | bytes 15080448 | tf_op jit(solution)/shard_map/dot_general | solution.py:39
  145.8 1.7 fusion.26
  147.5 4.1 %reshape.158 = bf16[8,64,16,80]{3,2,1,0:T(8,128)(2,1)S(1)} reshape(bf16[512,1280]{1,0:T(8,128)(2,1)} %get-tuple-element.9) | data formatting | bytes 2621440 | tf_op jit(solution)/shard_map/reshape | solution.py:48
  151.6 5.0 %reshape.159 = bf16[8,64,16,80]{3,2,1,0:T(8,128)(2,1)} reshape(bf16[512,1280]{1,0:T(8,128)(2,1)} %get-tuple-element.8) | data formatting | bytes 2621440 | tf_op jit(solution)/shard_map/reshape | solution.py:48
  156.7 4.1 %reshape.157 = bf16[8,64,16,80]{3,2,1,0:T(8,128)(2,1)} reshape(bf16[512,1280]{1,0:T(8,128)(2,1)S(1)} %get-tuple-element.7) | data formatting | bytes 2621440 | tf_op jit(solution)/shard_map/reshape | solution.py:48
  160.8 2.8 %fusion.7 = f32[8,16,64,64]{2,3,1,0:T(8,128)S(1)} fusion(bf16[8,64,16,80]{3,2,1,0:T(8,128)(2,1)} %reshape.159, bf16[8,64,16,80]{3,2,1,0:T(8,128)(2,1)S(1)} %reshape.158), kind=kOutput, calls=%fused_computation.19 | convolution fusion | flops 83886080 | bytes 4718592 | tf_op jit(solution)/shard_map/tqhd,tkhd->thqk/dot_general | solution.py:53
  163.6 1.5 fusion.27
  165.2 1.2 convolution_bitcast_fusion
  166.4 1.4 copy.45
  167.8 3.3 %reshape.160 = bf16[512,1280]{1,0:T(8,128)(2,1)} reshape(bf16[8,64,16,80]{3,2,1,0:T(8,128)(2,1)S(1)} %copy.45) | data formatting | bytes 2621440 | tf_op jit(solution)/shard_map/reshape | solution.py:66
  171.1 4.3 %multiply_reduce_fusion = (f32[512]{0:T(512)S(1)}, f32[512,1280]{1,0:T(8,128)S(1)}) fusion(bf16[1280,1280]{0,1:T(8,128)(2,1)} %all-gather.9.cloned.1.call-done, bf16[512,1280]{1,0:T(8,128)(2,1)} %reshape.160, pred[512]{0:T(512)(128)(4,1)S(1)} %iota_compare_fusion.3, bf16[512,1280]{1,0:T(8,128)(2,1)S(1)} %copy-done.2), kind=kOutput, calls=%fused_computation.15 | convolution fusion | flops 1680997888 | bytes 8522240 | tf_op jit(solution)/shard_map/dot_general | solution.py:69
  175.7 0.8 reshape_reshape.3
  176.6 1.8 copy.47
  178.3 5.5 %all-to-all-start.1 = ((bf16[16,8,5120]{2,0,1:T(8,128)(2,1)}), bf16[16,8,5120]{2,0,1:T(8,128)(2,1)S(1)}, u32[]{:S(2)}, u32[]{:S(2)}) async-start(bf16[16,8,5120]{2,0,1:T(8,128)(2,1)} %copy.47), calls=%async_computation.1 | async-start | bytes 2621440 | tf_op jit(solution)/shard_map/all_to_all | solution.py:99
  184.0 31.7 %all-to-all-done.1 = bf16[16,8,5120]{2,0,1:T(8,128)(2,1)S(1)} async-done(((bf16[16,8,5120]{2,0,1:T(8,128)(2,1)}), bf16[16,8,5120]{2,0,1:T(8,128)(2,1)S(1)}, u32[]{:S(2)}, u32[]{:S(2)}) %all-to-all-start.1) | async-done | bytes 1310752 | tf_op jit(solution)/shard_map/all_to_all | solution.py:99
  215.7 1.6 fusion.1
  (58 shorter events, 6.0 us)
Async XLA Ops:
  6.5 60.1 %all-gather.5.cloned.1.call-start = ((), (), s32[]{:S(2)}) async-start(), calls=%async_computation.2 | async-start | bytes 2949120 | tf_op jit(solution)/shard_map/all_gather | solution.py:38
  7.3 63.9 %copy-start.3 = (bf16[160,320]{1,0:T(8,128)(2,1)S(1)}, bf16[160,320]{1,0:T(8,128)(2,1)}, u32[]{:S(2)}) copy-start(bf16[160,320]{1,0:T(8,128)(2,1)} %param.11) | copy-start | bytes 307204
  7.3 129.0 %all-gather.7.cloned.1.call-start = ((), (), s32[]{:S(2)}) async-start(), calls=%async_computation.3 | async-start | bytes 12288000 | tf_op jit(solution)/shard_map/all_gather | solution.py:41
  71.0 34.4 %copy-start.8 = (s32[4]{0:T(128)S(1)}, s32[4]{0:T(128)}, u32[]{:S(2)}) copy-start(s32[4]{0:T(128)} %param.14) | copy-start | bytes 52
  71.0 35.1 %copy-start.6 = (s32[4]{0:T(128)S(1)}, s32[4]{0:T(128)}, u32[]{:S(2)}) copy-start(s32[4]{0:T(128)} %param.15) | copy-start | bytes 52
  71.0 35.4 %copy-start.9 = (u32[32]{0:T(128)S(1)}, u32[32]{0:T(128)}, u32[]{:S(2)}) copy-start(u32[32]{0:T(128)} %constant.61) | copy-start | bytes 388
  71.1 51.7 %copy-start.5 = (s32[512]{0:T(512)S(1)}, s32[512]{0:T(512)}, u32[]{:S(2)}) copy-start(s32[512]{0:T(512)} %param.13) | copy-start | bytes 6148
  71.1 53.1 %copy-start.1 = (bf16[512,1280]{1,0:T(8,128)(2,1)S(1)}, bf16[512,1280]{1,0:T(8,128)(2,1)}, u32[]{:S(2)}) copy-start(bf16[512,1280]{1,0:T(8,128)(2,1)} %param.8) | copy-start | bytes 3932164
  71.1 65.2 %copy-start.7 = (f32[1280]{0:T(1024)S(1)}, f32[1280]{0:T(1024)}, u32[]{:S(2)}) copy-start(f32[1280]{0:T(1024)} %param.9) | copy-start | bytes 15364
  71.1 99.9 %all-gather.9.cloned.1.call-start = ((), (), s32[]{:S(2)}) async-start(), calls=%async_computation.4 | async-start | bytes 4096000 | tf_op jit(solution)/shard_map/all_gather | solution.py:71
  118.2 60.2 %all-to-all-start = ((s32[16,8,1]{0,2,1:T(1,128)}), s32[16,8,1]{0,2,1:T(1,128)S(1)}, u32[]{:S(2)}, u32[]{:S(2)}) async-start(s32[16,8,1]{0,2,1:T(1,128)} %copy.39), calls=%async_computation | async-start | bytes 8192 | tf_op jit(solution)/shard_map/all_to_all | solution.py:100
  163.6 1.6 copy-start
  167.8 3.3 %copy-start.2 = (bf16[512,1280]{1,0:T(8,128)(2,1)S(1)}, bf16[512,1280]{1,0:T(8,128)(2,1)}, u32[]{:S(2)}) copy-start(bf16[512,1280]{1,0:T(8,128)(2,1)} %param.8) | copy-start | bytes 3932164
  171.1 4.4 %copy-start.4 = (f32[1280]{0:T(1024)S(1)}, f32[1280]{0:T(1024)}, u32[]{:S(2)}) copy-start(f32[1280]{0:T(1024)} %param.12) | copy-start | bytes 15364
  178.3 37.3 %all-to-all-start.1 = ((bf16[16,8,5120]{2,0,1:T(8,128)(2,1)}), bf16[16,8,5120]{2,0,1:T(8,128)(2,1)S(1)}, u32[]{:S(2)}, u32[]{:S(2)}) async-start(bf16[16,8,5120]{2,0,1:T(8,128)(2,1)} %copy.47), calls=%async_computation.1 | async-start | bytes 2621440 | tf_op jit(solution)/shard_map/all_to_all | solution.py:99
Sparse Core Ops, SparseCore 0:
  9.5 57.1 all-gather.4
  71.2 65.0 all-gather.6
  137.8 29.2 all-gather.8
where the time goes:
time: 224 us
  waiting for transfers between devices  103 us (46%)
  blocking collectives  41.6 us (19%)
  local copies, waits for them, and re-layouts  29.9 us (13%)
  matrix products  19.4 us (9%)
  between operations  14 us (6%)
  starting transfers between devices  10.1 us (5%)
  other arithmetic  5.32 us (2%)
    all_gather x1, waiting for transfers between devices, body(): qkv_rows = lax.all_gather(w_qkv, 'tensor', axis=0, tiled=True)  59.4 us
    all_gather x1, blocking collectives, body(): proj_rows = lax.all_gather(w_out, 'tensor', axis=0, tiled=True)  33 us
    all_to_all x1, waiting for transfers between devices, body(): lax.all_to_all(outgoing, 'tensor', split_axis=1, concat_axis=0, tiled=True)  31.7 us
    reshape x3, local copies, waits for them, and re-layouts, split_heads(): return block.reshape(tile_count, WINDOW, HEADS, head_width)  13.2 us
    all_gather x1, waiting for transfers between devices, body(): lax.all_gather(qkv_rows, 'pipe', axis=1, tiled=True)  11.6 us
    dot_general x1, matrix products, body(): jnp.dot(normed, lax.all_gather(qkv_rows, 'pipe', axis=1, tiled=True), pre...  9.49 us
    unnamed x1, blocking collectives  8.57 us
    all_to_all x1, starting transfers between devices, body(): lax.all_to_all(outgoing, 'tensor', split_axis=1, concat_axis=0, tiled=True)  5.51 us
  transfers between devices with their start and end apart: 5, of which 3 were waited for; matrix products, arithmetic and copies ran while one was open for 22% of the time, Pallas kernels for 0%

commit v1 on v0

--- a/solution.py
+++ b/solution.py
@@ -68,7 +68,9 @@
     proj_rows = lax.all_gather(w_out, "tensor", axis=0, tiled=True)
     attended = jnp.dot(
         context,
-        lax.all_gather(proj_rows, "pipe", axis=1, tiled=True),
+        jnp.concatenate(
+            lax.all_to_all(jnp.stack([proj_rows] * lax.axis_size("pipe")), "pipe", 0, 0), axis=1
+        ),
         preferred_element_type=jnp.float32,
     )
     hidden = residual + attended

time: 224 us -> 254 us (1.13)
  waiting for transfers between devices: 103 us -> 122 us
  starting transfers between devices: 10.1 us -> 19.7 us
    all_gather x1, waiting for transfers between devices: 11.6 us -> 31.2 us  [body(): lax.all_gather(qkv_rows, 'pipe', axis=1, tiled=True)]
    all_to_all x0 -> x1, starting transfers between devices: none -> 4.81 us  [body(): lax.all_to_all(jnp.stack([proj_rows] * lax.axis_size('pipe')), 'pipe', 0, 0)]
    convert_element_type x0 -> x2, local copies, waits for them, and re-layouts: none -> 4.64 us  [body(): context = jnp.where(live_row[:, None], context, 0.0).astype(jnp.bfloat16)]
    all_to_all x1, starting transfers between devices: 4.54 us -> 8.89 us  [body(): lax.all_to_all(outgoing_position, 'tensor', split_axis=1, concat_axis=0,...]
    reshape x1 -> x0, local copies, waits for them, and re-layouts: 3.27 us -> none  [body(): context = jnp.einsum('thqk,tkhd->tqhd', weights, values_tile, preferred_e...]
  transfers between devices with their start and end apart: 5 -> 5, of which waited for: 3 -> 3; matrix products, arithmetic and copies ran while one was open for 22% -> 19% of each run, Pallas kernels for 0% -> 0%
where the time goes in v1:
time: 254 us; the launch traced here: 253 us
  waiting for transfers between devices  122 us (48%)
  blocking collectives  41.4 us (16%)
  local copies, waits for them, and re-layouts  31 us (12%)
  starting transfers between devices  19.7 us (8%)
  matrix products  19.6 us (8%)
  between operations  14.2 us (6%)
  other arithmetic  4.66 us (2%)
    all_gather x1, waiting for transfers between devices, body(): qkv_rows = lax.all_gather(w_qkv, 'tensor', axis=0, tiled=True)  59.4 us
    all_gather x1, blocking collectives, body(): proj_rows = lax.all_gather(w_out, 'tensor', axis=0, tiled=True)  32.9 us
    all_gather x1, waiting for transfers between devices, body(): lax.all_gather(qkv_rows, 'pipe', axis=1, tiled=True)  31.2 us
    all_to_all x1, waiting for transfers between devices, body(): lax.all_to_all(outgoing, 'tensor', split_axis=1, concat_axis=0, tiled=True)  31.1 us
    reshape x3, local copies, waits for them, and re-layouts, split_heads(): return block.reshape(tile_count, WINDOW, HEADS, head_width)  13.2 us
    dot_general x1, matrix products, body(): jnp.dot(normed, lax.all_gather(qkv_rows, 'pipe', axis=1, tiled=True), pre...  9.49 us
    all_to_all x1, starting transfers between devices, body(): lax.all_to_all(outgoing_position, 'tensor', split_axis=1, concat_axis=0,...  8.89 us
    unnamed x1, blocking collectives  8.57 us
  transfers between devices with their start and end apart: 5, of which 3 were waited for; matrix products, arithmetic and copies ran while one was open for 19% of the time, Pallas kernels for 0%

profile of v1, /device:TPU:0, one launch (start us, length us, event | category | flops | bytes accessed | tf_op | source)
XLA Modules:
  0.0 253.1 jit_solution(16371545309001737180)
XLA Ops:
  7.3 59.4 %all-gather.4.cloned.1.call-done = bf16[1280,960]{1,0:T(8,128)(2,1)} async-done(((bf16[160,960]{1,0:T(8,128)(2,1)}), bf16[1280,960]{1,0:T(8,128)(2,1)}) %all-gather.4.cloned.1.call-update) | async-done | bytes 2457616 | tf_op jit(solution)/shard_map/all_gather | solution.py:38
  66.7 4.4 %copy.41 = bf16[1280,960]{0,1:T(8,128)(2,1)} copy(bf16[1280,960]{1,0:T(8,128)(2,1)} %all-gather.4.cloned.1.call-done) | data formatting | bytes 4915200 | tf_op jit(solution)/shard_map/all_gather | solution.py:38
  71.1 32.9 %all_gather.15 = bf16[1280,320]{1,0:T(8,128)(2,1)S(1)} all-gather(bf16[160,320]{1,0:T(8,128)(2,1)S(1)} %copy-done.3), channel_id=1, replica_groups=mesh['pipe'=4,'tensor'=8] {'tensor'}, dimensions={0}, use_global_device_ids=true | all-gather | bytes 921600 | tf_op jit(solution)/shard_map/all_gather | solution.py:68
  104.5 1.9 stack.2
  106.4 4.8 %all-to-all-start.1 = ((bf16[4,1280,320]{1,2,0:T(8,128)(2,1)}), bf16[4,1280,320]{1,2,0:T(8,128)(2,1)}, u32[]{:S(2)}, u32[]{:S(2)}) async-start(bf16[4,1280,320]{1,2,0:T(8,128)(2,1)} %stack.2), calls=%async_computation.1 | async-start | bytes 6553600 | tf_op jit(solution)/shard_map/all_to_all | solution.py:72
  113.6 8.6 %all-reduce = s32[64]{0:T(128)S(1)} all-reduce(s32[64]{0:T(128)S(1)} %dynamic-update-slice), channel_id=2, replica_groups=mesh['pipe'=4,'tensor'=8] {'tensor'}, use_global_device_ids=true, to_apply=%add | all-reduce | flops 64 | bytes 512
  125.1 31.2 %all-gather.6.cloned.1.call-done = bf16[1280,3840]{0,1:T(8,128)(2,1)} async-done(((bf16[1280,960]{0,1:T(8,128)(2,1)}), bf16[1280,3840]{0,1:T(8,128)(2,1)}) %all-gather.6.cloned.1.call-update) | async-done | bytes 9830416 | tf_op jit(solution)/shard_map/all_gather | solution.py:41
  156.3 9.5 %convolution_convert_fusion.1 = bf16[512,3840]{1,0:T(8,128)(2,1)S(1)} fusion(bf16[1280,3840]{0,1:T(8,128)(2,1)} %all-gather.6.cloned.1.call-done, bf16[512,1280]{1,0:T(8,128)(2,1)S(1)} %copy-done.1, f32[1280]{0:T(1024)S(1)} %copy-done.7, f32[512]{0:T(512)S(1)} %add_rsqrt_fusion.1), kind=kOutput, calls=%fused_computation.2 | convolution fusion | flops 5037752320 | bytes 15080448 | tf_op jit(solution)/shard_map/dot_general | solution.py:39
  165.8 1.7 fusion.26
  167.5 4.1 %reshape.171 = bf16[8,64,16,80]{3,2,1,0:T(8,128)(2,1)S(1)} reshape(bf16[512,1280]{1,0:T(8,128)(2,1)} %get-tuple-element.8) | data formatting | bytes 2621440 | tf_op jit(solution)/shard_map/reshape | solution.py:48
  171.6 5.0 %reshape.170 = bf16[8,64,16,80]{3,2,1,0:T(8,128)(2,1)} reshape(bf16[512,1280]{1,0:T(8,128)(2,1)} %get-tuple-element.9) | data formatting | bytes 2621440 | tf_op jit(solution)/shard_map/reshape | solution.py:48
  176.7 4.1 %reshape.169 = bf16[8,64,16,80]{3,2,1,0:T(8,128)(2,1)} reshape(bf16[512,1280]{1,0:T(8,128)(2,1)S(1)} %get-tuple-element.7) | data formatting | bytes 2621440 | tf_op jit(solution)/shard_map/reshape | solution.py:48
  180.7 2.8 %fusion.7 = f32[8,16,64,64]{2,3,1,0:T(8,128)S(1)} fusion(bf16[8,64,16,80]{3,2,1,0:T(8,128)(2,1)S(1)} %reshape.171, bf16[8,64,16,80]{3,2,1,0:T(8,128)(2,1)} %reshape.170), kind=kOutput, calls=%fused_computation.18 | convolution fusion | flops 83886080 | bytes 4718592 | tf_op jit(solution)/shard_map/tqhd,tkhd->thqk/dot_general | solution.py:53
  183.6 1.5 fusion.27
  185.2 1.4 fusion.14
  186.6 1.4 copy.46
  188.0 3.3 %convert_element_type.34 = bf16[512,1280]{1,0:T(8,128)(2,1)} reshape(bf16[8,64,16,80]{3,2,1,0:T(8,128)(2,1)S(1)} %copy.46) | data formatting | bytes 2621440 | tf_op jit(solution)/shard_map/convert_element_type | solution.py:67
  191.3 8.9 %all-to-all-start = ((s32[16,8,1]{0,2,1:T(1,128)}), s32[16,8,1]{0,2,1:T(1,128)S(1)}, u32[]{:S(2)}, u32[]{:S(2)}) async-start(s32[16,8,1]{0,2,1:T(1,128)} %copy.40), calls=%async_computation | async-start | bytes 8192 | tf_op jit(solution)/shard_map/all_to_all | solution.py:102
  200.2 4.4 %multiply_reduce_fusion = (f32[512]{0:T(512)S(1)}, f32[512,1280]{1,0:T(8,128)S(1)}) fusion(bf16[512,1280]{1,0:T(8,128)(2,1)} %convert_element_type.34, bf16[1280,1280]{0,1:T(8,128)(2,1)} %bitcast.6, bf16[512,1280]{1,0:T(8,128)(2,1)S(1)} %copy-done.2), kind=kOutput, calls=%fused_computation.16 | convolution fusion | flops 1680342528 | bytes 8521728 | tf_op jit(solution)/shard_map/dot_general | solution.py:69
  204.8 0.8 reshape_reshape.3
  205.7 1.8 copy.48
  207.5 6.0 %all-to-all-start.2 = ((bf16[16,8,5120]{2,0,1:T(8,128)(2,1)}), bf16[16,8,5120]{2,0,1:T(8,128)(2,1)S(1)}, u32[]{:S(2)}, u32[]{:S(2)}) async-start(bf16[16,8,5120]{2,0,1:T(8,128)(2,1)} %copy.48), calls=%async_computation.2 | async-start | bytes 2621440 | tf_op jit(solution)/shard_map/all_to_all | solution.py:101
  213.6 31.1 %all-to-all-done.2 = bf16[16,8,5120]{2,0,1:T(8,128)(2,1)S(1)} async-done(((bf16[16,8,5120]{2,0,1:T(8,128)(2,1)}), bf16[16,8,5120]{2,0,1:T(8,128)(2,1)S(1)}, u32[]{:S(2)}, u32[]{:S(2)}) %all-to-all-start.2) | async-done | bytes 1310752 | tf_op jit(solution)/shard_map/all_to_all | solution.py:101
  244.7 1.6 fusion.1
  (57 shorter events, 6.5 us)
Async XLA Ops:
  6.5 60.1 %all-gather.4.cloned.1.call-start = ((), (), s32[]{:S(2)}) async-start(), calls=%async_computation.3 | async-start | bytes 2949120 | tf_op jit(solution)/shard_map/all_gather | solution.py:38
  7.3 63.8 %copy-start.3 = (bf16[160,320]{1,0:T(8,128)(2,1)S(1)}, bf16[160,320]{1,0:T(8,128)(2,1)}, u32[]{:S(2)}) copy-start(bf16[160,320]{1,0:T(8,128)(2,1)} %param.11) | copy-start | bytes 307204
  7.3 149.0 %all-gather.6.cloned.1.call-start = ((), (), s32[]{:S(2)}) async-start(), calls=%async_computation.4 | async-start | bytes 12288000 | tf_op jit(solution)/shard_map/all_gather | solution.py:41
  106.4 4.9 %copy-start.5 = (s32[512]{0:T(512)S(1)}, s32[512]{0:T(512)}, u32[]{:S(2)}) copy-start(s32[512]{0:T(512)} %param.13) | copy-start | bytes 6148
  106.4 4.9 %copy-start.8 = (s32[4]{0:T(128)S(1)}, s32[4]{0:T(128)}, u32[]{:S(2)}) copy-start(s32[4]{0:T(128)} %param.14) | copy-start | bytes 52
  106.4 5.8 %copy-start.9 = (u32[32]{0:T(128)S(1)}, u32[32]{0:T(128)}, u32[]{:S(2)}) copy-start(u32[32]{0:T(128)} %constant.62) | copy-start | bytes 388
  106.4 6.9 %copy-start.6 = (s32[4]{0:T(128)S(1)}, s32[4]{0:T(128)}, u32[]{:S(2)}) copy-start(s32[4]{0:T(128)} %param.15) | copy-start | bytes 52
  106.4 18.1 %copy-start.1 = (bf16[512,1280]{1,0:T(8,128)(2,1)S(1)}, bf16[512,1280]{1,0:T(8,128)(2,1)}, u32[]{:S(2)}) copy-start(bf16[512,1280]{1,0:T(8,128)(2,1)} %param.8) | copy-start | bytes 3932164
  106.4 49.8 %copy-start.7 = (f32[1280]{0:T(1024)S(1)}, f32[1280]{0:T(1024)}, u32[]{:S(2)}) copy-start(f32[1280]{0:T(1024)} %param.9) | copy-start | bytes 15364
  106.4 84.8 %all-to-all-start.1 = ((bf16[4,1280,320]{1,2,0:T(8,128)(2,1)}), bf16[4,1280,320]{1,2,0:T(8,128)(2,1)}, u32[]{:S(2)}, u32[]{:S(2)}) async-start(bf16[4,1280,320]{1,2,0:T(8,128)(2,1)} %stack.2), calls=%async_computation.1 | async-start | bytes 6553600 | tf_op jit(solution)/shard_map/all_to_all | solution.py:72
  183.6 1.6 copy-start
  188.0 12.2 %copy-start.2 = (bf16[512,1280]{1,0:T(8,128)(2,1)S(1)}, bf16[512,1280]{1,0:T(8,128)(2,1)}, u32[]{:S(2)}) copy-start(bf16[512,1280]{1,0:T(8,128)(2,1)} %param.8) | copy-start | bytes 3932164
  191.3 16.2 %all-to-all-start = ((s32[16,8,1]{0,2,1:T(1,128)}), s32[16,8,1]{0,2,1:T(1,128)S(1)}, u32[]{:S(2)}, u32[]{:S(2)}) async-start(s32[16,8,1]{0,2,1:T(1,128)} %copy.40), calls=%async_computation | async-start | bytes 8192 | tf_op jit(solution)/shard_map/all_to_all | solution.py:102
  200.2 4.4 %copy-start.4 = (f32[1280]{0:T(1024)S(1)}, f32[1280]{0:T(1024)}, u32[]{:S(2)}) copy-start(f32[1280]{0:T(1024)} %param.12) | copy-start | bytes 15364
  207.5 37.2 %all-to-all-start.2 = ((bf16[16,8,5120]{2,0,1:T(8,128)(2,1)}), bf16[16,8,5120]{2,0,1:T(8,128)(2,1)S(1)}, u32[]{:S(2)}, u32[]{:S(2)}) async-start(bf16[16,8,5120]{2,0,1:T(8,128)(2,1)} %copy.48), calls=%async_computation.2 | async-start | bytes 2621440 | tf_op jit(solution)/shard_map/all_to_all | solution.py:101
Sparse Core Ops, SparseCore 0:
  9.5 57.1 all-gather.3
  71.2 85.0 all-gather.5
